TPU v7x, 32 devices: a whole 2x2x4 slice. The times are simulated.
32 devices in a mesh: dp: 4 (over x, y), tp: 8 (over z, core).
Axes of the slice: x: 2, y: 2, z: 4, core: 2. Of those that a mesh axis runs over, the one named last changes fastest.
Arguments:
- hidden: bfloat16 [4, 128, 5120], P('dp', 'tp'), parts along dimension 0
- norm_attn: float32 [2, 5120], replicated
- w_q: bfloat16 [2, 5120, 40, 128], P(None, None, 'tp')
- w_kv: bfloat16 [2, 5120, 2, 8, 128], replicated
- w_o: bfloat16 [2, 40, 128, 5120], P(None, 'tp')
- norm_mlp: float32 [2, 5120], replicated
- w_gate: bfloat16 [2, 5120, 13824], P(None, None, 'tp')
- w_up: bfloat16 [2, 5120, 13824], P(None, None, 'tp')
- w_down: bfloat16 [2, 13824, 5120], P(None, 'tp')
Outputs:
- output: bfloat16 [4, 128, 5120], P('dp', 'tp'), parts along dimension 0
There are 4 independent parts. A program takes and returns all parts, laid end to end along the dimension named above; an argument that names none is the same for every part.
All inputs are finite; a program needn't handle non-finite values.
Results may differ from a plain program's by a relative error of at most 0.0109612.
Values are sent between devices in bfloat16 or wider.
A program may use at most 1 GiB of HBM per device.

v0:
```python
import math
import jax
import jax.numpy as jnp
from jax import lax
from jax.sharding import PartitionSpec as P

EPS = 1e-5
ROPE_BASE = 10000.0


def rms_norm(resid, gain):
    mean_sq = jnp.mean(resid * resid, axis=-1, keepdims=True)
    return (resid * lax.rsqrt(mean_sq + EPS) * gain).astype(jnp.bfloat16)


def rope_tables(positions, head_dim):
    half_dim = head_dim // 2
    inv_freq = jnp.power(ROPE_BASE, -2.0 * jnp.arange(half_dim, dtype=jnp.float32) / head_dim)
    angles = positions.astype(jnp.float32)[:, None] * inv_freq[None, :]
    return jnp.cos(angles), jnp.sin(angles)


def apply_rope(proj, cos_t, sin_t):
    half_dim = proj.shape[-1] // 2
    first_half = proj[..., :half_dim]
    second_half = proj[..., half_dim:]
    cos_b = cos_t[None, :, None, :]
    sin_b = sin_t[None, :, None, :]
    return jnp.concatenate([first_half * cos_b - second_half * sin_b, second_half * cos_b + first_half * sin_b], axis=-1)


def solution(mesh):
    n_tp = mesh.shape['tp']
    tok_spec = P('dp', 'tp', None)
    in_specs = (tok_spec, P(), P(None, None, 'tp', None), P(), P(None, 'tp', None, None), P(), P(None, None, 'tp'), P(None, None, 'tp'), P(None, 'tp', None))

    def gather_rows(normed):
        return lax.all_gather(normed, 'tp', axis=1, tiled=True)

    def reduce_rows(partial):
        batch_loc, seq_len, width = partial.shape
        blocks = partial.astype(jnp.bfloat16).reshape(batch_loc, n_tp, seq_len // n_tp, width)
        received = lax.all_to_all(blocks, 'tp', 1, 1)
        return jnp.sum(received, axis=1, dtype=jnp.float32)

    def body(hidden, norm_attn, w_q, w_kv, w_o, norm_mlp, w_gate, w_up, w_down):
        n_layers = w_q.shape[0]
        heads_loc = w_q.shape[2]
        head_dim = w_q.shape[3]
        n_kv = w_kv.shape[3]
        kv_loc = max(1, n_kv // n_tp)
        group_loc = heads_loc // kv_loc
        batch_loc, rows_loc, _ = hidden.shape
        seq_len = rows_loc * n_tp
        kv_start = (lax.axis_index('tp') * n_kv) // n_tp
        positions = jnp.arange(seq_len)
        cos_t, sin_t = rope_tables(positions, head_dim)
        causal_mask = positions[:, None] >= positions[None, :]
        inv_sqrt = 1.0 / math.sqrt(head_dim)
        resid = hidden.astype(jnp.float32)
        for layer_idx in range(n_layers):
            gathered = gather_rows(rms_norm(resid, norm_attn[layer_idx]))
            kv_weight = lax.dynamic_slice_in_dim(w_kv[layer_idx], kv_start, kv_loc, axis=2)
            q_proj = jnp.einsum('bsd,dhe->bshe', gathered, w_q[layer_idx], preferred_element_type=jnp.float32)
            kv_proj = jnp.einsum('bsd,dcke->bscke', gathered, kv_weight, preferred_element_type=jnp.float32)
            queries = apply_rope(q_proj, cos_t, sin_t).astype(jnp.bfloat16).reshape(batch_loc, seq_len, kv_loc, group_loc, head_dim)
            keys = apply_rope(kv_proj[:, :, 0], cos_t, sin_t).astype(jnp.bfloat16)
            values = kv_proj[:, :, 1].astype(jnp.bfloat16)
            scores = jnp.einsum('bqkgd,bskd->bkgqs', queries, keys, preferred_element_type=jnp.float32) * inv_sqrt
            scores = jnp.where(causal_mask, scores, -jnp.inf)
            attn_probs = jax.nn.softmax(scores, axis=-1).astype(jnp.bfloat16)
            context = jnp.einsum('bkgqs,bskd->bqkgd', attn_probs, values, preferred_element_type=jnp.float32).astype(jnp.bfloat16)
            context = context.reshape(batch_loc, seq_len, heads_loc, head_dim)
            partial = jnp.einsum('bqhd,hdf->bqf', context, w_o[layer_idx], preferred_element_type=jnp.float32)
            resid = resid + reduce_rows(partial)
            gathered = gather_rows(rms_norm(resid, norm_mlp[layer_idx]))
            gate_proj = jnp.einsum('bsd,df->bsf', gathered, w_gate[layer_idx], preferred_element_type=jnp.float32)
            up_proj = jnp.einsum('bsd,df->bsf', gathered, w_up[layer_idx], preferred_element_type=jnp.float32)
            activated = (jax.nn.silu(gate_proj) * up_proj).astype(jnp.bfloat16)
            partial = jnp.einsum('bsf,fd->bsd', activated, w_down[layer_idx], preferred_element_type=jnp.float32)
            resid = resid + reduce_rows(partial)
        return resid.astype(jnp.bfloat16)

    return jax.shard_map(body, mesh=mesh, in_specs=in_specs, out_specs=tok_spec, check_vma=False)
```

profile of v0, /device:TPU:0, one launch (start us, length us, event | category | flops | bytes accessed | tf_op | source)
XLA Modules:
  0.0 395.9 jit_solution(14627600382650818729)
XLA Ops:
  6.5 0.9 fusion.142
  7.4 1.1 fusion.82
  8.5 1.7 fusion.84
  10.2 28.8 %fusion.140 = (bf16[1,5120,2,8,128]{4,3,2,1,0:T(8,128)(2,1)}, bf16[1,5120,2,8,128]{4,3,2,1,0:T(8,128)(2,1)}) fusion(bf16[2,5120,2,8,128]{4,3,2,1,0:T(8,128)(2,1)} %param.12), kind=kLoop, calls=%fused_computation.151 | loop fusion | bytes 83886080 | tf_op jit(solution)/shard_map/slice | solution.py:63
  39.0 22.1 %constant_dynamic-slice_fusion = (bf16[1,5120,2,1,128]{4,3,2,1,0:T(2,128)(2,1)}, bf16[1,5120,2,1,128]{4,3,2,1,0:T(2,128)(2,1)}) fusion(bf16[1,5120,2,8,128]{4,3,2,1,0:T(8,128)(2,1)} %get-tuple-element.7, s32[]{:T(128)S(6)} %select_n.17, bf16[1,5120,2,8,128]{4,3,2,1,0:T(8,128)(2,1)} %get-tuple-element.8), kind=kLoop, calls=%fused_computation.144 | loop fusion | bytes 10485764 | tf_op jit(solution)/shard_map/dynamic_slice | solution.py:63
  61.1 9.6 %copy.22 = bf16[1,5120,2,1,128]{1,4,2,3,0:T(8,128)(2,1)S(1)} copy(bf16[1,5120,2,1,128]{4,3,2,1,0:T(2,128)(2,1)} %get-tuple-element.30) | data formatting | bytes 5242880 | tf_op jit(solution)/shard_map/dynamic_slice | solution.py:63
  70.7 10.4 %fusion.141 = (bf16[1,5120,5,128]{3,1,2,0:T(8,128)(2,1)}, bf16[1,5120,5,128]{3,1,2,0:T(8,128)(2,1)}) fusion(bf16[2,5120,5,128]{3,1,2,0:T(8,128)(2,1)} %param.11), kind=kLoop, calls=%fused_computation.152 | loop fusion | bytes 26214400 | tf_op jit(solution)/shard_map/slice | solution.py:64
  81.1 9.5 %copy.48 = bf16[1,5120,5,128]{1,3,2,0:T(8,128)(2,1)} copy(bf16[1,5120,5,128]{3,1,2,0:T(8,128)(2,1)} %get-tuple-element.10) | data formatting | bytes 13107200
  90.6 0.2 multiply_cosine_fusion
  90.9 2.2 fusion.64
  93.0 0.2 fusion.135
  93.3 5.1 %fusion.62 = f32[128,640]{0,1:S(1)} fusion(bf16[5120,640]{0,1:T(8,128)(2,1)} %bitcast.226, bf16[1,128,5120]{2,1,0:T(8,128)(2,1)} %all-gather.5.cloned.1.call-done), kind=kOutput, calls=%fused_computation.46 | convolution fusion | flops 838860800 | bytes 8192000
  98.4 0.2 fusion.144
  98.7 0.1 fusion.86
  98.8 5.3 %fusion.39 = bf16[128,5120]{1,0:T(8,128)(2,1)} fusion(bf16[2,5,128,5120]{3,2,1,0:T(8,128)(2,1)} %param.13, f32[1,1,5,128,128]{3,4,2,1,0:T(8,128)S(1)} %get-tuple-element.26, f32[5,128]{1,0:T(8,128)S(1)} %fusion.86, f32[5,128]{1,0:T(8,128)S(1)} %get-tuple-element.25, f32[1,128,2,1,128]{1,4,2,3,0:T(8,128)S(1)} %bitcast.238), kind=kOutput, calls=%fused_computation.29 | convolution fusion | flops 860815360 | bytes 8232960 | tf_op jit(solution)/shard_map/bqhd,hdf->bqf/dot_general | solution.py:74
  104.1 6.4 %all-to-all-start = ((bf16[1,8,16,5120]{3,2,0,1:T(8,128)(2,1)}), bf16[1,8,16,5120]{3,2,0,1:T(8,128)(2,1)S(1)}, u32[]{:S(2)}, u32[]{:S(2)}) async-start(bf16[1,8,16,5120]{3,2,0,1:T(8,128)(2,1)} %bitcast.29), calls=%async_computation | async-start | bytes 2621440 | tf_op jit(solution)/shard_map/all_to_all | solution.py:43
  110.6 31.9 %all-to-all-done = bf16[1,8,16,5120]{3,2,0,1:T(8,128)(2,1)S(1)} async-done(((bf16[1,8,16,5120]{3,2,0,1:T(8,128)(2,1)}), bf16[1,8,16,5120]{3,2,0,1:T(8,128)(2,1)S(1)}, u32[]{:S(2)}, u32[]{:S(2)}) %all-to-all-start) | async-done | bytes 1310752 | tf_op jit(solution)/shard_map/all_to_all | solution.py:43
  142.5 0.2 convert_reduce_fusion.3
  142.7 0.2 multiply_reduce_fusion.2
  142.9 0.8 multiply_convert_fusion.2
  143.7 0.2 all-gather.9.cloned.1.call-start
  143.9 22.3 %all-gather.7.cloned.1.call-done = bf16[1,128,5120]{2,1,0:T(8,128)(2,1)} async-done(((bf16[1,16,5120]{2,1,0:T(8,128)(2,1)}), bf16[1,128,5120]{2,1,0:T(8,128)(2,1)}) %all-gather.7.cloned.1.call-update) | async-done | bytes 1310736 | tf_op jit(solution)/shard_map/all_gather | solution.py:38
  166.3 8.9 %fusion.10 = f32[128,1728]{0,1:T(8,128)S(1)} fusion(bf16[2,5120,1728]{1,2,0:T(8,128)(2,1)} %param.15, bf16[1,128,5120]{2,1,0:T(8,128)(2,1)} %all-gather.7.cloned.1.call-done), kind=kOutput, calls=%fused_computation.10 | convolution fusion | flops 2264924160 | bytes 19890176 | tf_op jit(solution)/shard_map/bsd,df->bsf/dot_general | solution.py:77
  175.1 19.3 %fusion.30 = bf16[128,5120]{1,0:T(8,128)(2,1)S(1)} fusion(bf16[2,1728,5120]{2,1,0:T(8,128)(2,1)} %param.17, bf16[2,5120,1728]{1,2,0:T(8,128)(2,1)} %param.16, bf16[1,128,5120]{2,1,0:T(8,128)(2,1)} %all-gather.7.cloned.1.call-done, f32[128,1728]{0,1:T(8,128)S(1)} %fusion.10), kind=kOutput, calls=%fused_computation.26 | convolution fusion | flops 4531830784 | bytes 38895616 | tf_op jit(solution)/shard_map/bsf,fd->bsd/dot_general | solution.py:80
  194.5 35.4 %all_to_all.20 = bf16[1,8,16,5120]{3,2,0,1:T(8,128)(2,1)S(1)} all-to-all(bf16[1,8,16,5120]{3,2,0,1:T(8,128)(2,1)S(1)} %bitcast.233), channel_id=1, replica_groups=mesh['dp'=4,'tp'=8] {'tp'}, dimensions={1} | all-to-all | bytes 2621440 | tf_op jit(solution)/shard_map/all_to_all | solution.py:43
  229.9 0.2 convert_reduce_fusion.2
  230.0 0.2 multiply_reduce_fusion.1
  230.2 0.8 multiply_convert_fusion.1
  231.0 0.0 all-gather.11.cloned.1.call-start
  231.1 9.6 %copy.30 = bf16[1,5120,2,1,128]{1,4,2,3,0:T(8,128)(2,1)S(1)} copy(bf16[1,5120,2,1,128]{4,3,2,1,0:T(2,128)(2,1)} %get-tuple-element.29) | data formatting | bytes 5242880 | tf_op jit(solution)/shard_map/dynamic_slice | solution.py:63
  240.7 9.5 %copy.49 = bf16[1,5120,5,128]{1,3,2,0:T(8,128)(2,1)} copy(bf16[1,5120,5,128]{3,1,2,0:T(8,128)(2,1)} %get-tuple-element.9) | data formatting | bytes 13107200
  250.2 3.4 all-gather.9.cloned.1.call-done
  253.6 2.2 fusion.58
  255.8 0.2 fusion.133
  256.0 5.1 %fusion.56 = f32[128,640]{0,1:S(1)} fusion(bf16[5120,640]{0,1:T(8,128)(2,1)} %bitcast.227, bf16[1,128,5120]{2,1,0:T(8,128)(2,1)} %all-gather.9.cloned.1.call-done), kind=kOutput, calls=%fused_computation.40 | convolution fusion | flops 838860800 | bytes 8192000
  261.2 0.2 fusion.145
  261.4 0.1 fusion.87
  261.5 4.2 %fusion.36 = bf16[128,5120]{1,0:T(8,128)(2,1)S(1)} fusion(bf16[2,5,128,5120]{3,2,1,0:T(8,128)(2,1)} %param.13, f32[1,1,5,128,128]{3,4,2,1,0:T(8,128)S(1)} %get-tuple-element.28, f32[5,128]{1,0:T(8,128)S(1)} %fusion.87, f32[5,128]{1,0:T(8,128)S(1)} %get-tuple-element.27, f32[1,128,2,1,128]{1,4,3,2,0:T(8,128)S(1)} %bitcast.236), kind=kOutput, calls=%fused_computation.28 | convolution fusion | flops 860815360 | bytes 8232960 | tf_op jit(solution)/shard_map/bqhd,hdf->bqf/dot_general | solution.py:74
  265.7 35.4 %all_to_all.21 = bf16[1,8,16,5120]{3,2,0,1:T(8,128)(2,1)S(1)} all-to-all(bf16[1,8,16,5120]{3,2,0,1:T(8,128)(2,1)S(1)} %bitcast.232), channel_id=1, replica_groups=mesh['dp'=4,'tp'=8] {'tp'}, dimensions={1} | all-to-all | bytes 2621440 | tf_op jit(solution)/shard_map/all_to_all | solution.py:43
  301.1 0.2 convert_reduce_fusion.1
  301.3 0.2 multiply_reduce_fusion
  301.5 0.8 multiply_convert_fusion
  302.3 22.6 %all-gather.11.cloned.1.call-done = bf16[1,128,5120]{2,1,0:T(8,128)(2,1)} async-done(((bf16[1,16,5120]{2,1,0:T(8,128)(2,1)}), bf16[1,128,5120]{2,1,0:T(8,128)(2,1)}) %all-gather.11.cloned.1.call-update) | async-done | bytes 1310736 | tf_op jit(solution)/shard_map/all_gather | solution.py:38
  324.8 8.9 %fusion.4 = f32[128,1728]{0,1:T(8,128)S(1)} fusion(bf16[2,5120,1728]{1,2,0:T(8,128)(2,1)} %param.15, bf16[1,128,5120]{2,1,0:T(8,128)(2,1)} %all-gather.11.cloned.1.call-done), kind=kOutput, calls=%fused_computation.4 | convolution fusion | flops 2264924160 | bytes 19890176 | tf_op jit(solution)/shard_map/bsd,df->bsf/dot_general | solution.py:77
  333.7 19.3 %fusion.33 = bf16[128,5120]{1,0:T(8,128)(2,1)S(1)} fusion(bf16[2,1728,5120]{2,1,0:T(8,128)(2,1)} %param.17, bf16[2,5120,1728]{1,2,0:T(8,128)(2,1)} %param.16, bf16[1,128,5120]{2,1,0:T(8,128)(2,1)} %all-gather.11.cloned.1.call-done, f32[128,1728]{0,1:T(8,128)S(1)} %fusion.4), kind=kOutput, calls=%fused_computation.27 | convolution fusion | flops 4531830784 | bytes 38895616 | tf_op jit(solution)/shard_map/bsf,fd->bsd/dot_general | solution.py:80
  353.0 35.4 %all_to_all.22 = bf16[1,8,16,5120]{3,2,0,1:T(8,128)(2,1)S(1)} all-to-all(bf16[1,8,16,5120]{3,2,0,1:T(8,128)(2,1)S(1)} %bitcast.234), channel_id=1, replica_groups=mesh['dp'=4,'tp'=8] {'tp'}, dimensions={1} | all-to-all | bytes 2621440 | tf_op jit(solution)/shard_map/all_to_all | solution.py:43
  388.4 0.2 convert_reduce_fusion
  388.6 0.7 fusion.85
  (23 shorter events, 0.3 us)
Async XLA Ops:
  6.5 84.3 %all-gather.5.cloned.1.call-start = ((), (), s32[]{:S(2)}) async-start(), calls=%async_computation.4 | async-start | bytes 1474560 | tf_op jit(solution)/shard_map/all_gather | solution.py:38
  98.8 11.8 %copy-start.1 = (f32[2,5120]{1,0:T(2,128)S(1)}, f32[2,5120]{1,0:T(2,128)}, u32[]{:S(2)}) copy-start(f32[2,5120]{1,0:T(2,128)} %param.14) | copy-start | bytes 122884
  98.8 43.9 %copy-start = (bf16[1,16,5120]{2,1,0:T(8,128)(2,1)S(1)}, bf16[1,16,5120]{2,1,0:T(8,128)(2,1)}, u32[]{:S(2)}) copy-start(bf16[1,16,5120]{2,1,0:T(8,128)(2,1)} %param.9) | copy-start | bytes 491524
  104.1 38.4 %all-to-all-start = ((bf16[1,8,16,5120]{3,2,0,1:T(8,128)(2,1)}), bf16[1,8,16,5120]{3,2,0,1:T(8,128)(2,1)S(1)}, u32[]{:S(2)}, u32[]{:S(2)}) async-start(bf16[1,8,16,5120]{3,2,0,1:T(8,128)(2,1)} %bitcast.29), calls=%async_computation | async-start | bytes 2621440 | tf_op jit(solution)/shard_map/all_to_all | solution.py:43
  110.5 55.8 %all-gather.7.cloned.1.call-start = ((), (), s32[]{:S(2)}) async-start(), calls=%async_computation.5 | async-start | bytes 1474560 | tf_op jit(solution)/shard_map/all_gather | solution.py:38
  143.7 109.9 %all-gather.9.cloned.1.call-start = ((), (), s32[]{:S(2)}) async-start(), calls=%async_computation.6 | async-start | bytes 1474560 | tf_op jit(solution)/shard_map/all_gather | solution.py:38
  231.0 93.8 %all-gather.11.cloned.1.call-start = ((), (), s32[]{:S(2)}) async-start(), calls=%async_computation.7 | async-start | bytes 1474560 | tf_op jit(solution)/shard_map/all_gather | solution.py:38
Sparse Core Ops, SparseCore 0:
  10.3 26.3 all-gather.4
  143.8 22.3 all-gather.6
  231.1 22.4 all-gather.8
  302.4 22.4 all-gather.10
where the time goes:
time: 397 us; the launch traced here: 396 us
  blocking collectives  106 us (27%)
  local copies, waits for them, and re-layouts  100 us (25%)
  matrix products  81 us (20%)
  waiting for transfers between devices  80.3 us (20%)
  between operations  13.4 us (3%)
  other arithmetic  7.89 us (2%)
  starting transfers between devices  6.68 us (2%)
    all_to_all x3, blocking collectives, reduce_rows(): received = lax.all_to_all(blocks, 'tp', 1, 1)  106 us
    all_gather x4, waiting for transfers between devices, gather_rows(): return lax.all_gather(normed, 'tp', axis=1, tiled=True)  48.3 us
    dynamic_slice x3, local copies, waits for them, and re-layouts, body(): lax.dynamic_slice_in_dim(w_kv[layer_idx], kv_start, kv_loc, axis=2)  41.3 us
    dot_general x2, matrix products, body(): jnp.einsum('bsf,fd->bsd', activated, w_down[layer_idx], preferred_element...  38.6 us
    all_to_all x1, waiting for transfers between devices, reduce_rows(): received = lax.all_to_all(blocks, 'tp', 1, 1)  31.9 us
    slice x1, local copies, waits for them, and re-layouts, body(): w_kv[layer_idx]  28.8 us
    unnamed x6, local copies, waits for them, and re-layouts  19 us
    dot_general x2, matrix products, body(): jnp.einsum('bsd,df->bsf', gathered, w_gate[layer_idx], preferred_element_...  17.7 us
  transfers between devices with their start and end apart: 5, of which 4 were waited for; matrix products, arithmetic and copies ran while one was open for 25% of the time, Pallas kernels for 0%

commit v1 on v0

v1 whole, which is shorter than its diff:
```python
import functools
import math
import jax
import jax.numpy as jnp
from jax import lax
from jax.experimental import pallas as pl
from jax.experimental.pallas import tpu as pltpu
from jax.sharding import PartitionSpec as P

EPS = 1e-5
ROPE_BASE = 10000.0
MESH = pl.DeviceIdType.MESH
NZ = 4
LANES = 128


class Cfg:
    def __init__(self, layers, seq, width, heads, head, ff):
        self.L, self.S, self.D, self.H, self.E, self.F = layers, seq, width, heads, head, ff
        self.T = seq // 8
        self.CK = 512
        self.NK = width // self.CK
        self.CN = 512
        self.NN = width // self.CN
        self.NG = 5
        self.ND = 4
        self.NR = 3
        self.SUB = 128
        self.AHEAD = 3


def kernel(cfg, hid_ref, na_ref, nm_ref, cos_ref, sin_ref, mask_ref,
           wq_hbm, wkv_hbm, wo_hbm, wg_hbm, wu_hbm, wd_hbm, out_ref,
           xg, rsd, rsb, stg_d, stg_o, qb, resid, wqkv, raw, scr, wo_b, gu_b, wd_b,
           qkv, gacc, uacc, act, ctx,
           s_wq, s_kv, s_wo, s_gu, s_wd,
           r_dir, r_par, s_own, s_far, s_par,
           q_par, q_dir, t_par, t_dir):
    c = cfg
    L, S, D, H, E, T = c.L, c.S, c.D, c.H, c.E, c.T
    HS = S // 2
    dp = lax.axis_index("dp")
    tp = lax.axis_index("tp")
    z = tp // 2
    core = lax.rem(tp, 2)
    partner = tp + 1 - 2 * core
    middle = jnp.logical_or(z == 1, z == 2)
    far = jnp.where(z == 1, 3, 0)
    near = jnp.where(z == 1, 0, 3)

    def chip(zz):
        return 2 * zz + core

    def rcopy(src, dst, ss, rs, to):
        return pltpu.make_async_remote_copy(src_ref=src, dst_ref=dst, send_sem=ss, recv_sem=rs,
                                            device_id=(dp, to), device_id_type=MESH)

    def blk(zz, base=0):
        return pl.ds(pl.multiple_of(base + zz * T, T), T)

    def kcols(k):
        return pl.ds(pl.multiple_of(k * c.CK, c.CK), c.CK)

    def ncols(j):
        return pl.ds(pl.multiple_of(j * c.CN, c.CN), c.CN)

    def wq_copy(l, h):
        return pltpu.make_async_copy(wq_hbm.at[l, h], wqkv.at[:, pl.ds(h * E, E)], s_wq.at[h])

    pair = pl.multiple_of(2 * (tp // 2), 2)

    def kv_copy(g):
        l, k, slot = g // c.NK, lax.rem(g, c.NK), lax.rem(g, c.NR)
        return pltpu.make_async_copy(
            wkv_hbm.at[l, pl.ds(pl.multiple_of(k * c.CK, c.CK), c.CK), :, pl.ds(pair, 2)],
            raw.at[slot], s_kv.at[slot])

    def wo_copy(l):
        return pltpu.make_async_copy(wo_hbm.at[l], wo_b, s_wo)

    def gu_copies(g):
        l, k, slot = g // c.NK, lax.rem(g, c.NK), lax.rem(g, c.NG)
        return [pltpu.make_async_copy(w.at[l, :, kcols(k)], gu_b.at[slot, i], s_gu.at[slot, i])
                for i, w in enumerate((wg_hbm, wu_hbm))]

    def wd_copy(g):
        l, j, slot = g // c.NN, lax.rem(g, c.NN), lax.rem(g, c.ND)
        return pltpu.make_async_copy(wd_hbm.at[l, :, ncols(j)], wd_b.at[slot], s_wd.at[slot])

    for h in range(H):
        wq_copy(0, h).start()
    for g in range(c.NR):
        kv_copy(g).start()

    bar = pltpu.get_barrier_semaphore()
    pl.semaphore_signal(bar, inc=1, device_id=(dp, partner), device_id_type=MESH)
    for d in range(1, NZ):
        pl.semaphore_signal(bar, inc=1, device_id=(dp, chip(lax.rem(z + d, NZ))), device_id_type=MESH)
    pl.semaphore_wait(bar, NZ)

    def gather_phase(l, ph, compute):
        buf = xg.at[l, ph]

        def own(k):
            src = buf.at[blk(z), kcols(k)]
            res = [(None, rcopy(src, buf.at[blk(z, HS), kcols(k)], s_own.at[0, k], r_par.at[l, ph, z, k], partner))]
            for i, dz in enumerate((2, -2, 1, -1)):
                ok = jnp.logical_and(z + dz >= 0, z + dz < NZ)
                to = chip(jnp.clip(z + dz, 0, NZ - 1))
                res.append((ok, rcopy(src, src, s_own.at[1 + i, k], r_dir.at[l, ph, z, k], to)))
            return res

        def dir_in(o, k):
            b = buf.at[blk(o), kcols(k)]
            return rcopy(b, b, s_far.at[k], r_dir.at[l, ph, o, k], partner)

        def far_send(k):
            b = buf.at[blk(far), kcols(k)]
            return rcopy(b, b, s_far.at[k], r_dir.at[l, ph, far, k], chip(near))

        def par_send(o, k):
            return rcopy(buf.at[blk(o), kcols(k)], buf.at[blk(o, HS), kcols(k)],
                         s_par.at[o, k], r_par.at[l, ph, o, k], partner)

        def start_own(k):
            for ok, cp in own(k):
                if ok is None:
                    cp.start()
                else:
                    @pl.when(ok)
                    def _(cp=cp):
                        cp.start()

        def stage_far(k):
            @pl.when(middle)
            def _():
                dir_in(far, k).wait_recv()
                far_send(k).start()

        def stage_par(k):
            for o in range(NZ):
                @pl.when(jnp.logical_and(o != z, jnp.logical_not(jnp.logical_and(middle, o == far))))
                def _(o=o):
                    dir_in(o, k).wait_recv()
                    par_send(o, k).start()

                @pl.when(jnp.logical_and(middle, o == far))
                def _(o=o):
                    par_send(o, k).start()

        def stage_in(k):
            for o in range(NZ):
                par_send(o, k).wait_recv()

        for k in range(min(c.AHEAD, c.NK)):
            start_own(k)

        def step(i, _):
            @pl.when(i + c.AHEAD < c.NK)
            def _():
                start_own(i + c.AHEAD)

            @pl.when(i < c.NK)
            def _():
                stage_far(i)

            @pl.when(jnp.logical_and(i >= 1, i < c.NK + 1))
            def _():
                stage_par(i - 1)

            @pl.when(i >= 2)
            def _():
                stage_in(i - 2)
                compute(i - 2)
            return 0

        lax.fori_loop(0, c.NK + 2, step, 0)

        def drain(k, _):
            for ok, cp in own(k):
                if ok is None:
                    cp.wait_send()
                else:
                    @pl.when(ok)
                    def _(cp=cp):
                        cp.wait_send()

            @pl.when(middle)
            def _():
                far_send(k).wait_send()
            for o in range(NZ):
                @pl.when(o != z)
                def _(o=o):
                    par_send(o, k).wait_send()
            return 0

        lax.fori_loop(0, c.NK, drain, 0)

    def reduce_phase(l, ph, produce):
        def par(j):
            return rcopy(stg_d.at[:, ncols(j)], rsd.at[l, ph, :, ncols(j)], t_par.at[j], q_par.at[l, ph, j], partner)

        def out(d, j):
            is_far = (z == 0) if d == 3 else (z == 3)
            if d in (0, 3):
                mid = 1 if d == 3 else 2
                to = jnp.where(is_far, mid, d)
                slot = jnp.where(is_far, mid, z)
                ok = jnp.logical_or(z == 0, z == 2) if d == 3 else jnp.logical_or(z == 1, z == 3)
            else:
                to, slot, ok = d, z, z != d
            return ok, rcopy(stg_o.at[blk(d), ncols(j)], rsb.at[l, ph, slot, :, ncols(j)],
                             t_dir.at[d, j], q_dir.at[l, ph, slot, j], chip(to))

        def mid_send(j):
            return rcopy(stg_o.at[blk(far), ncols(j)], rsb.at[l, ph, z, :, ncols(j)],
                         t_dir.at[far, j], q_dir.at[l, ph, z, j], chip(far))

        def dir_in(slot, j):
            b = rsb.at[l, ph, slot, :, ncols(j)]
            return rcopy(b, b, t_dir.at[0, j], q_dir.at[l, ph, slot, j], partner)

        def stage_make(j):
            part = produce(j)
            qb[:, ncols(j)] = part[:HS]
            stg_d[:, ncols(j)] = part[HS:].astype(jnp.bfloat16)
            par(j).start()

        def stage_pair(j):
            par(j).wait_recv()
            both = qb[:, ncols(j)] + rsd[l, ph, :, ncols(j)].astype(jnp.float32)
            qb[:, ncols(j)] = both
            stg_o[:, ncols(j)] = both.astype(jnp.bfloat16)
            for d in (3, 0, 2, 1):
                ok, cp = out(d, j)

                @pl.when(ok)
                def _(cp=cp):
                    cp.start()

        def stage_mid(j):
            @pl.when(middle)
            def _():
                dir_in(z, j).wait_recv()
                both = qb[blk(far), ncols(j)] + rsb[l, ph, z, :, ncols(j)].astype(jnp.float32)
                stg_o[blk(far), ncols(j)] = both.astype(jnp.bfloat16)
                mid_send(j).start()

        def stage_sum(j):
            resid[:, ncols(j)] = resid[:, ncols(j)] + qb[blk(z), ncols(j)]
            for s in range(NZ):
                dist = jnp.abs(z - s)

                @pl.when(jnp.logical_and(dist >= 1, dist <= 2))
                def _(s=s):
                    dir_in(s, j).wait_recv()
                    resid[:, ncols(j)] = resid[:, ncols(j)] + rsb[l, ph, s, :, ncols(j)].astype(jnp.float32)

        def step(i, _):
            @pl.when(i < c.NN)
            def _():
                stage_make(i)

            @pl.when(jnp.logical_and(i >= 1, i < c.NN + 1))
            def _():
                stage_pair(i - 1)

            @pl.when(jnp.logical_and(i >= 2, i < c.NN + 2))
            def _():
                stage_mid(i - 2)

            @pl.when(i >= 4)
            def _():
                stage_sum(i - 4)
            return 0

        lax.fori_loop(0, c.NN + 4, step, 0)

        def drain(j, _):
            par(j).wait_send()
            for d in range(NZ):
                ok, cp = out(d, j)

                @pl.when(ok)
                def _(cp=cp):
                    cp.wait_send()

            @pl.when(middle)
            def _():
                mid_send(j).wait_send()
            return 0

        lax.fori_loop(0, c.NN, drain, 0)

    def norm_into(l, ph, gain_ref):
        r = resid[...]
        inv = lax.rsqrt(jnp.mean(r * r, axis=-1, keepdims=True) + EPS)
        xg[l, ph, blk(z), :] = (r * inv * gain_ref[l]).astype(jnp.bfloat16)

    def rope(x):
        return x * cos_ref[...] + pltpu.roll(x, E // 2, 1) * sin_ref[...]

    def attention():
        inv_sqrt = 1.0 / math.sqrt(E)
        keys = rope(qkv[:, H * E:(H + 1) * E]).astype(jnp.bfloat16)
        values = qkv[:, (H + 1) * E:].astype(jnp.bfloat16)
        keep = mask_ref[...] > 0.5
        for h in range(H):
            q = rope(qkv[:, h * E:(h + 1) * E]).astype(jnp.bfloat16)
            s = lax.dot_general(q, keys, (((1,), (1,)), ((), ())), preferred_element_type=jnp.float32) * inv_sqrt
            s = jnp.where(keep, s, -jnp.inf)
            e = jnp.exp(s - jnp.max(s, axis=-1, keepdims=True))
            p = (e / jnp.sum(e, axis=-1, keepdims=True)).astype(jnp.bfloat16)
            ctx[:, h * E:(h + 1) * E] = jnp.dot(p, values, preferred_element_type=jnp.float32).astype(jnp.bfloat16)

    resid[...] = hid_ref[...].astype(jnp.float32)
    par_head = lax.rem(tp, 2)

    def layer(l, _):
        norm_into(l, 0, na_ref)

        def qkv_chunk(k):
            @pl.when(k == 0)
            def _():
                for h in range(H):
                    wq_copy(l, h).wait()
                qkv[...] = jnp.zeros_like(qkv)

            @pl.when(jnp.logical_and(l == 0, k == 0))
            def _():
                wo_copy(0).start()
            for n in range(c.NG):
                @pl.when(jnp.logical_and(l == 0, k == 1 + n))
                def _(n=n):
                    for cp in gu_copies(n):
                        cp.start()
            for n in range(c.ND):
                @pl.when(jnp.logical_and(l == 0, k == 1 + c.NG + n))
                def _(n=n):
                    wd_copy(n).start()
            g = l * c.NK + k
            kv_copy(g).wait()
            slot = lax.rem(g, c.NR)

            def sub(s, _):
                r0 = pl.multiple_of(s * c.SUB, c.SUB)
                scr[...] = raw[slot, pl.ds(r0, c.SUB)].astype(jnp.float32).reshape(c.SUB * 4, LANES)
                for i in range(2):
                    y = scr[pl.ds(2 * i + par_head, c.SUB, stride=4), :]
                    wqkv[pl.ds(pl.multiple_of(k * c.CK + r0, c.SUB), c.SUB),
                         (H + i) * E:(H + 1 + i) * E] = y.astype(jnp.bfloat16)
                return 0

            lax.fori_loop(0, c.CK // c.SUB, sub, 0)

            @pl.when(g + c.NR < L * c.NK)
            def _():
                kv_copy(g + c.NR).start()
            rows = pl.ds(pl.multiple_of(k * c.CK, c.CK), c.CK)
            qkv[...] += jnp.dot(xg[l, 0, :, kcols(k)], wqkv[rows, :], preferred_element_type=jnp.float32)

        gather_phase(l, 0, qkv_chunk)

        @pl.when(l + 1 < L)
        def _():
            for h in range(H):
                wq_copy(l + 1, h).start()
        attention()
        wo_copy(l).wait()
        reduce_phase(l, 0, lambda j: jnp.dot(ctx[...], wo_b[:, ncols(j)], preferred_element_type=jnp.float32))

        @pl.when(l + 1 < L)
        def _():
            wo_copy(l + 1).start()
        norm_into(l, 1, nm_ref)

        def gu_chunk(k):
            @pl.when(k == 0)
            def _():
                gacc[...] = jnp.zeros_like(gacc)
                uacc[...] = jnp.zeros_like(uacc)
            g = l * c.NK + k
            slot = lax.rem(g, c.NG)
            x = xg[l, 1, :, kcols(k)]
            for i, (cp, acc) in enumerate(zip(gu_copies(g), (gacc, uacc))):
                cp.wait()
                acc[...] += lax.dot_general(x, gu_b[slot, i], (((1,), (1,)), ((), ())),
                                            preferred_element_type=jnp.float32)

            @pl.when(g + c.NG < L * c.NK)
            def _():
                for cp in gu_copies(g + c.NG):
                    cp.start()

        gather_phase(l, 1, gu_chunk)
        gate = gacc[...]
        act[...] = (gate * jax.nn.sigmoid(gate) * uacc[...]).astype(jnp.bfloat16)

        def down_chunk(j):
            g = l * c.NN + j
            slot = lax.rem(g, c.ND)
            wd_copy(g).wait()
            part = jnp.dot(act[...], wd_b[slot], preferred_element_type=jnp.float32)

            @pl.when(g + c.ND < L * c.NN)
            def _():
                wd_copy(g + c.ND).start()
            return part

        reduce_phase(l, 1, down_chunk)
        return 0

    lax.fori_loop(0, L, layer, 0)
    out_ref[...] = resid[...].astype(jnp.bfloat16)


def solution(mesh):
    tok_spec = P('dp', 'tp', None)
    in_specs = (tok_spec, P(), P(None, None, 'tp', None), P(), P(None, 'tp', None, None), P(), P(None, None, 'tp'), P(None, None, 'tp'), P(None, 'tp', None))

    def body(hidden, norm_attn, w_q, w_kv, w_o, norm_mlp, w_gate, w_up, w_down):
        L, D, H, E = w_q.shape
        F = w_gate.shape[2]
        T = hidden.shape[1]
        S = 8 * T
        cfg = Cfg(L, S, D, H, E, F)
        core = lax.rem(lax.axis_index('tp'), 2)
        row = jnp.arange(S)
        cls = jnp.where(row < S // 2, core, 1 - core)
        pos = ((row % (S // 2)) // T) * (2 * T) + cls * T + row % T
        inv_freq = jnp.power(ROPE_BASE, -2.0 * jnp.arange(E // 2, dtype=jnp.float32) / E)
        ang = pos.astype(jnp.float32)[:, None] * inv_freq[None, :]
        cos_t, sin_t = jnp.cos(ang), jnp.sin(ang)
        cos_f = jnp.concatenate([cos_t, cos_t], axis=1)
        sin_f = jnp.concatenate([-sin_t, sin_t], axis=1)
        mask = (pos[:, None] >= pos[None, :]).astype(jnp.float32)

        c = cfg
        bf, f32 = jnp.bfloat16, jnp.float32
        vm = pl.BlockSpec(memory_space=pltpu.VMEM)
        hb = pl.BlockSpec(memory_space=pl.ANY)
        dma = pltpu.SemaphoreType.DMA
        scratch = [
            pltpu.VMEM((L, 2, S, D), bf),
            pltpu.VMEM((L, 2, S // 2, D), bf),
            pltpu.VMEM((L, 2, NZ, T, D), bf),
            pltpu.VMEM((S // 2, D), bf),
            pltpu.VMEM((S // 2, D), bf),
            pltpu.VMEM((S // 2, D), f32),
            pltpu.VMEM((T, D), f32),
            pltpu.VMEM((D, (H + 2) * E), bf),
            pltpu.VMEM((c.NR, c.CK, 2, 2, E), bf),
            pltpu.VMEM((c.SUB * 4, E), f32),
            pltpu.VMEM((H * E, D), bf),
            pltpu.VMEM((c.NG, 2, F, c.CK), bf),
            pltpu.VMEM((c.ND, F, c.CN), bf),
            pltpu.VMEM((S, (H + 2) * E), f32),
            pltpu.VMEM((S, F), f32),
            pltpu.VMEM((S, F), f32),
            pltpu.VMEM((S, F), bf),
            pltpu.VMEM((S, H * E), bf),
            dma((H,)), dma((c.NR,)), dma, dma((c.NG, 2)), dma((c.ND,)),
            dma((L, 2, NZ, c.NK)), dma((L, 2, NZ, c.NK)), dma((5, c.NK)), dma((c.NK,)), dma((NZ, c.NK)),
            dma((L, 2, c.NN)), dma((L, 2, NZ, c.NN)), dma((c.NN,)), dma((NZ, c.NN)),
        ]
        out = pl.pallas_call(
            functools.partial(kernel, cfg),
            out_shape=jax.ShapeDtypeStruct((T, D), bf),
            in_specs=[vm] * 6 + [hb] * 6,
            out_specs=vm,
            scratch_shapes=scratch,
            compiler_params=pltpu.CompilerParams(collective_id=0, has_side_effects=True, vmem_limit_bytes=67043328),
            name="layers",
        )(hidden[0], norm_attn.reshape(L, 1, D), norm_mlp.reshape(L, 1, D), cos_f, sin_f, mask,
          jnp.transpose(w_q, (0, 2, 1, 3)), w_kv, w_o.reshape(L, H * E, D),
          jnp.transpose(w_gate, (0, 2, 1)), jnp.transpose(w_up, (0, 2, 1)), w_down)
        return out[None]

    return jax.shard_map(body, mesh=mesh, in_specs=in_specs, out_specs=tok_spec, check_vma=False)
```

time: 397 us -> 197 us (0.50)
  Pallas kernels: 0 us -> 190 us
  blocking collectives: 106 us -> 0 us
  local copies, waits for them, and re-layouts: 100 us -> 4.43 us
  matrix products: 81 us -> 0 us
  waiting for transfers between devices: 80.3 us -> 0 us
  between operations: 13.4 us -> 0.02 us
  starting transfers between devices: 6.68 us -> 0 us
  other arithmetic: 7.89 us -> 1.8 us
    pallas_call x0 -> x1, Pallas kernels: none -> 190 us  [body(): pl.pallas_call(functools.partial(kernel, cfg), out_shape=jax.ShapeDtypeSt...]
    all_to_all x3 -> x0, blocking collectives: 106 us -> none  [reduce_rows(): received = lax.all_to_all(blocks, 'tp', 1, 1)]
    dot_general x8 -> x0, matrix products: 66.4 us -> none  [the longest x2 38.6 us: body(): jnp.einsum('bsf,fd->bsd', activated, w_down[layer_idx], preferred_element...]
    all_gather x4 -> x0, waiting for transfers between devices: 48.3 us -> none  [gather_rows(): return lax.all_gather(normed, 'tp', axis=1, tiled=True)]
    dynamic_slice x3 -> x0, local copies, waits for them, and re-layouts: 41.3 us -> none  [body(): lax.dynamic_slice_in_dim(w_kv[layer_idx], kv_start, kv_loc, axis=2)]
    slice x4 -> x0, local copies, waits for them, and re-layouts: 40.1 us -> none  [the longest x1 28.8 us: body(): w_kv[layer_idx]]
    all_to_all x1 -> x0, waiting for transfers between devices: 31.9 us -> none  [reduce_rows(): received = lax.all_to_all(blocks, 'tp', 1, 1)]
    unnamed x6 -> x1, local copies, waits for them, and re-layouts: 19 us -> 1.59 us
  transfers between devices with their start and end apart: 5 -> 0, of which waited for: 4 -> 0; matrix products, arithmetic and copies ran while one was open for 25% -> 0% of each run, Pallas kernels for 0% -> 0%
where the time goes in v1:
time: 197 us; the launch traced here: 196 us
  Pallas kernels  190 us (96%)
  local copies, waits for them, and re-layouts  4.43 us (2%)
    pallas_call x1, Pallas kernels, body(): pl.pallas_call(functools.partial(kernel, cfg), out_shape=jax.ShapeDtypeSt...  190 us

profile of v1, /device:TPU:0, one launch (start us, length us, event | category | flops | bytes accessed | tf_op | source)
XLA Modules:
  0.0 196.4 jit_solution(12680720093048219711)
XLA Ops:
  0.0 0.3 fusion
  0.3 0.8 pad_maximum_fusion
  1.1 0.7 compare_convert_fusion.mask_ref
  1.8 1.4 reshape.93.na_ref
  3.2 1.4 reshape.94.nm_ref
  4.6 190.1 %layers.1 = bf16[16,5120]{1,0:T(8,128)(2,1)} custom-call(bf16[16,5120]{1,0:T(8,128)(2,1)} %bitcast.11, f32[2,1,5120]{2,1,0:T(1,128)} %reshape.93.na_ref, f32[2,1,5120]{2,1,0:T(1,128)} %reshape.94.nm_ref, f32[128,128]{1,0:T(8,128)} %get-tuple-element.10.cos_ref, f32[128,128]{1,0:T(8,128)} %get-tuple-element.11.sin_ref, ...), custom_call_target="tpu_custom_call" | custom-call | tf_op jit(solution)/shard_map/layers/pallas_call | solution.py:466
  194.8 1.6 copy.11
  (2 shorter events, 0.0 us)

commit v2 on v1

v2 whole, which is shorter than its diff:
```python
import functools
import math
import jax
import jax.numpy as jnp
from jax import lax
from jax.experimental import pallas as pl
from jax.experimental.pallas import tpu as pltpu
from jax.sharding import PartitionSpec as P

EPS = 1e-5
ROPE_BASE = 10000.0
MESH = pl.DeviceIdType.MESH
NZ = 4
LANES = 128


class Cfg:
    def __init__(self, layers, seq, width, heads, head, ff):
        self.L, self.S, self.D, self.H, self.E, self.F = layers, seq, width, heads, head, ff
        self.T = seq // 8
        self.CKS = (1280, 1024)
        self.NKS = tuple(width // n for n in self.CKS)
        self.KC = 512
        self.NC = width // self.KC
        self.FP = -(-ff // LANES) * LANES
        self.CN = 1024
        self.NN = width // self.CN
        self.NG = 2
        self.ND = 2
        self.NR = 3
        self.SUB = 128
        self.AHEAD = (4, 3)
        self.LF, self.LP, self.LC = 0, 1, 2
        self.RP, self.RA, self.RB, self.RM, self.RS = 2, 3, 4, 4, 6


def kernel(cfg, hid_hbm, na_hbm, nm_hbm, wq_hbm, wkv_hbm, wo_hbm, wg_hbm, wu_hbm, wd_hbm, out_ref,
           xg, rsd, rsb, stg_d, stg_o, qb, resid, wqkv, raw, scr, wo_b, gu_b, wd_b,
           qkv, gacc, act, ctx, hid_ref, na_ref, nm_ref, cos_ref, sin_ref, mask_ref, s_in,
           s_wq, s_kv, s_wo, s_gu, s_wd,
           r_dir, r_par, s_own, s_far, s_near, s_par,
           q_par, q_dir, t_par, t_dir):
    c = cfg
    L, S, D, H, E, T = c.L, c.S, c.D, c.H, c.E, c.T
    HS = S // 2
    dp = lax.axis_index("dp")
    tp = lax.axis_index("tp")
    z = tp // 2
    core = lax.rem(tp, 2)
    partner = tp + 1 - 2 * core
    middle = jnp.logical_or(z == 1, z == 2)
    far = jnp.where(z == 1, 3, 0)
    near = jnp.where(z == 1, 0, 3)

    def chip(zz):
        return 2 * zz + core

    def rcopy(src, dst, ss, rs, to):
        return pltpu.make_async_remote_copy(src_ref=src, dst_ref=dst, send_sem=ss, recv_sem=rs,
                                            device_id=(dp, to), device_id_type=MESH)

    def blk(zz, base=0):
        return pl.ds(pl.multiple_of(base + zz * T, T), T)

    def kcols(ph, k):
        return pl.ds(pl.multiple_of(k * c.CKS[ph], c.CKS[ph]), c.CKS[ph])

    def ncols(j):
        return pl.ds(pl.multiple_of(j * c.CN, c.CN), c.CN)

    def wq_copy(l, h):
        return pltpu.make_async_copy(wq_hbm.at[l, h], wqkv.at[:, pl.ds(h * E, E)], s_wq.at[h])

    pair = pl.multiple_of(2 * (tp // 2), 2)

    def kv_copy(g):
        l, k, slot = g // c.NC, lax.rem(g, c.NC), lax.rem(g, c.NR)
        return pltpu.make_async_copy(
            wkv_hbm.at[l, pl.ds(pl.multiple_of(k * c.KC, c.KC), c.KC), :, pl.ds(pair, 2)],
            raw.at[slot], s_kv.at[slot])

    def wo_copy(l):
        return pltpu.make_async_copy(wo_hbm.at[l], wo_b, s_wo)

    def gu_copies(g):
        l, k, slot = g // c.NKS[1], lax.rem(g, c.NKS[1]), lax.rem(g, c.NG)
        return [pltpu.make_async_copy(w.at[l, :, kcols(1, k)], gu_b.at[slot, pl.ds(i * c.FP, c.F)], s_gu.at[slot, i])
                for i, w in enumerate((wg_hbm, wu_hbm))]

    def wd_copy(g):
        l, j, slot = g // c.NN, lax.rem(g, c.NN), lax.rem(g, c.ND)
        return pltpu.make_async_copy(wd_hbm.at[l, :, ncols(j)], wd_b.at[slot], s_wd.at[slot])

    bar = pltpu.get_barrier_semaphore()
    pl.semaphore_signal(bar, inc=1, device_id=(dp, partner), device_id_type=MESH)
    for d in range(1, NZ):
        pl.semaphore_signal(bar, inc=1, device_id=(dp, chip(lax.rem(z + d, NZ))), device_id_type=MESH)

    inputs = [pltpu.make_async_copy(a, b, s_in.at[i])
              for i, (a, b) in enumerate(((hid_hbm, hid_ref), (na_hbm, na_ref), (nm_hbm, nm_ref)))]
    for cp in inputs:
        cp.start()
    for g in range(c.NR):
        kv_copy(g).start()
    for h in range(H):
        wq_copy(0, h).start()

    def gather_phase(l, ph, compute, before=None):
        buf = xg.at[l, ph]
        nk = c.NKS[ph]

        def own(k):
            src = buf.at[blk(z), kcols(ph, k)]
            res = [(None, rcopy(src, buf.at[blk(z, HS), kcols(ph, k)], s_own.at[0, k], r_par.at[l, ph, z, k], partner))]
            for i, dz in enumerate((2, -2, 1, -1)):
                ok = jnp.logical_and(z + dz >= 0, z + dz < NZ)
                if abs(dz) == 1:
                    late = jnp.logical_and(middle, z + dz == near)
                    ok = jnp.logical_and(ok, jnp.logical_not(late))
                to = chip(jnp.clip(z + dz, 0, NZ - 1))
                res.append((ok, rcopy(src, src, s_own.at[1 + i, k], r_dir.at[l, ph, z, k], to)))
            return res

        def near_send(k):
            b = buf.at[blk(z), kcols(ph, k)]
            return rcopy(b, b, s_near.at[k], r_dir.at[l, ph, z, k], chip(near))

        def dir_in(o, k):
            b = buf.at[blk(o), kcols(ph, k)]
            return rcopy(b, b, s_far.at[k], r_dir.at[l, ph, o, k], partner)

        def far_send(k):
            b = buf.at[blk(far), kcols(ph, k)]
            return rcopy(b, b, s_far.at[k], r_dir.at[l, ph, far, k], chip(near))

        def par_send(o, k):
            return rcopy(buf.at[blk(o), kcols(ph, k)], buf.at[blk(o, HS), kcols(ph, k)],
                         s_par.at[o, k], r_par.at[l, ph, o, k], partner)

        def start_own(k):
            for ok, cp in own(k):
                if ok is None:
                    cp.start()
                else:
                    @pl.when(ok)
                    def _(cp=cp):
                        cp.start()

        def stage_far(k):
            @pl.when(middle)
            def _():
                dir_in(far, k).wait_recv()
                far_send(k).start()
                near_send(k).start()

        def stage_par(k):
            for o in range(NZ):
                @pl.when(jnp.logical_and(o != z, jnp.logical_not(jnp.logical_and(middle, o == far))))
                def _(o=o):
                    dir_in(o, k).wait_recv()
                    par_send(o, k).start()

                @pl.when(jnp.logical_and(middle, o == far))
                def _(o=o):
                    par_send(o, k).start()

        def stage_in(k):
            for o in range(NZ):
                par_send(o, k).wait_recv()

        ahead = min(c.AHEAD[ph], nk)
        for k in range(ahead):
            start_own(k)

        if before is not None:
            before()

        def step(i, _):
            if ahead < nk:
                @pl.when(i + ahead < nk)
                def _():
                    start_own(i + ahead)

            @pl.when(jnp.logical_and(i >= c.LF, i < nk + c.LF))
            def _():
                stage_far(i - c.LF)

            @pl.when(jnp.logical_and(i >= c.LP, i < nk + c.LP))
            def _():
                stage_par(i - c.LP)

            @pl.when(i >= c.LC)
            def _():
                stage_in(i - c.LC)
                compute(i - c.LC)
            return 0

        lax.fori_loop(0, nk + c.LC, step, 0)

        def drain(k, _):
            for ok, cp in own(k):
                if ok is None:
                    cp.wait_send()
                else:
                    @pl.when(ok)
                    def _(cp=cp):
                        cp.wait_send()

            @pl.when(middle)
            def _():
                far_send(k).wait_send()
                near_send(k).wait_send()
            for o in range(NZ):
                @pl.when(o != z)
                def _(o=o):
                    par_send(o, k).wait_send()
            return 0

        lax.fori_loop(0, nk, drain, 0)

    def reduce_phase(l, ph, produce, beside=None):
        def par(j):
            return rcopy(stg_d.at[:, ncols(j)], rsd.at[l, ph, :, ncols(j)], t_par.at[j], q_par.at[l, ph, j], partner)

        def out(d, j):
            is_far = (z == 0) if d == 3 else (z == 3)
            if d in (0, 3):
                mid = 1 if d == 3 else 2
                to = jnp.where(is_far, mid, d)
                slot = jnp.where(is_far, mid, z)
                ok = jnp.logical_or(z == 0, z == 2) if d == 3 else jnp.logical_or(z == 1, z == 3)
            else:
                to, slot, ok = d, z, z != d
            return ok, rcopy(stg_o.at[blk(d), ncols(j)], rsb.at[l, ph, slot, :, ncols(j)],
                             t_dir.at[d, j], q_dir.at[l, ph, slot, j], chip(to))

        def mid_send(j):
            return rcopy(stg_o.at[blk(far), ncols(j)], rsb.at[l, ph, z, :, ncols(j)],
                         t_dir.at[far, j], q_dir.at[l, ph, z, j], chip(far))

        def dir_in(slot, j):
            b = rsb.at[l, ph, slot, :, ncols(j)]
            return rcopy(b, b, t_dir.at[0, j], q_dir.at[l, ph, slot, j], partner)

        def stage_make(j):
            part = produce(j)
            qb[:, ncols(j)] = part[:HS]
            stg_d[:, ncols(j)] = part[HS:].astype(jnp.bfloat16)
            par(j).start()

        def send(j, order, which):
            for d in order:
                ok, cp = out(d, j)

                @pl.when(jnp.logical_and(ok, which(d)))
                def _(cp=cp):
                    cp.start()

        def stage_pair(j):
            par(j).wait_recv()
            both = qb[:, ncols(j)] + rsd[l, ph, :, ncols(j)].astype(jnp.float32)
            qb[:, ncols(j)] = both
            stg_o[:, ncols(j)] = both.astype(jnp.bfloat16)
            send(j, (3, 0, 2, 1), lambda d: jnp.logical_or(middle, z == 3 - d) if d in (0, 3) else middle)

        def stage_mid(j):
            @pl.when(middle)
            def _():
                dir_in(z, j).wait_recv()
                both = qb[blk(far), ncols(j)] + rsb[l, ph, z, :, ncols(j)].astype(jnp.float32)
                stg_o[blk(far), ncols(j)] = both.astype(jnp.bfloat16)
                mid_send(j).start()

        def stage_sum(j):
            resid[:, ncols(j)] = resid[:, ncols(j)] + qb[blk(z), ncols(j)]
            for s in range(NZ):
                dist = jnp.abs(z - s)

                @pl.when(jnp.logical_and(dist >= 1, dist <= 2))
                def _(s=s):
                    dir_in(s, j).wait_recv()
                    resid[:, ncols(j)] = resid[:, ncols(j)] + rsb[l, ph, s, :, ncols(j)].astype(jnp.float32)

        def step(i, _):
            @pl.when(i < c.NN)
            def _():
                stage_make(i)

            @pl.when(jnp.logical_and(i >= c.RP, i < c.NN + c.RP))
            def _():
                stage_pair(i - c.RP)

            if beside is not None:
                beside(i)

            @pl.when(jnp.logical_and(i >= c.RA, i < c.NN + c.RA))
            def _():
                send(i - c.RA, (2, 1), lambda d: z == (0 if d == 2 else 3))

            @pl.when(jnp.logical_and(i >= c.RB, i < c.NN + c.RB))
            def _():
                send(i - c.RB, (1, 2), lambda d: z == (0 if d == 1 else 3))

            @pl.when(jnp.logical_and(i >= c.RM, i < c.NN + c.RM))
            def _():
                stage_mid(i - c.RM)

            @pl.when(i >= c.RS)
            def _():
                stage_sum(i - c.RS)
            return 0

        lax.fori_loop(0, c.NN + c.RS, step, 0)

        def drain(j, _):
            par(j).wait_send()
            for d in range(NZ):
                ok, cp = out(d, j)

                @pl.when(ok)
                def _(cp=cp):
                    cp.wait_send()

            @pl.when(middle)
            def _():
                mid_send(j).wait_send()
            return 0

        lax.fori_loop(0, c.NN, drain, 0)

    def norm_into(l, ph, gain_ref):
        r = resid[...]
        inv = lax.rsqrt(jnp.mean(r * r, axis=-1, keepdims=True) + EPS)
        xg[l, ph, blk(z), :] = (r * inv * gain_ref[pl.ds(l, 1), :]).astype(jnp.bfloat16)

    def rope(x):
        return x * cos_ref[...] + pltpu.roll(x, E // 2, 1) * sin_ref[...]

    def attention():
        inv_sqrt = 1.0 / math.sqrt(E)
        keys = rope(qkv[:, H * E:(H + 1) * E]).astype(jnp.bfloat16)
        values = qkv[:, (H + 1) * E:].astype(jnp.bfloat16)
        keep = mask_ref[...] > 0.5
        for h in range(H):
            q = rope(qkv[:, h * E:(h + 1) * E]).astype(jnp.bfloat16)
            s = lax.dot_general(q, keys, (((1,), (1,)), ((), ())), preferred_element_type=jnp.float32) * inv_sqrt
            s = jnp.where(keep, s, -jnp.inf)
            e = jnp.exp(s - jnp.max(s, axis=-1, keepdims=True))
            p = (e / jnp.sum(e, axis=-1, keepdims=True)).astype(jnp.bfloat16)
            ctx[:, h * E:(h + 1) * E] = jnp.dot(p, values, preferred_element_type=jnp.float32).astype(jnp.bfloat16)

    par_head = lax.rem(tp, 2)

    def kv_take(l, k):
        g = l * c.NC + k
        kv_copy(g).wait()
        slot = lax.rem(g, c.NR)

        def sub(s, _):
            r0 = pl.multiple_of(s * c.SUB, c.SUB)
            scr[...] = raw[slot, pl.ds(r0, c.SUB)].astype(jnp.float32).reshape(c.SUB * 4, LANES)
            for i in range(2):
                y = scr[pl.ds(2 * i + par_head, c.SUB, stride=4), :]
                wqkv[pl.ds(pl.multiple_of(k * c.KC + r0, c.SUB), c.SUB),
                     (H + i) * E:(H + 1 + i) * E] = y.astype(jnp.bfloat16)
            return 0

        lax.fori_loop(0, c.KC // c.SUB, sub, 0)

        @pl.when(g + c.NR < L * c.NC)
        def _():
            kv_copy(g + c.NR).start()

    def tables():
        def position(row):
            cls = jnp.where(row < HS, core, 1 - core)
            return (lax.shift_right_logical(row & (HS - 1), T.bit_length() - 1) * (2 * T)
                    + cls * T + (row & (T - 1)))

        pos = position(lax.broadcasted_iota(jnp.int32, (S, E), 0))
        lane = lax.broadcasted_iota(jnp.int32, (S, E), 1)
        pair_i = (lane & (E // 2 - 1)).astype(jnp.float32)
        ang = pos.astype(jnp.float32) * jnp.exp(pair_i * (-2.0 * math.log(ROPE_BASE) / E))
        cos_ref[...] = jnp.cos(ang)
        sin = jnp.sin(ang)
        sin_ref[...] = jnp.where(lane < E // 2, -sin, sin)
        kpos = position(lax.broadcasted_iota(jnp.int32, (S, S), 1))
        qpos = position(lax.broadcasted_iota(jnp.int32, (S, S), 0))
        mask_ref[...] = jnp.where(qpos >= kpos, 1.0, 0.0)

    gu_b[:, c.F:c.FP, :] = jnp.zeros((c.NG, c.FP - c.F, c.CKS[1]), jnp.bfloat16)
    for cp in inputs:
        cp.wait()
    resid[...] = hid_ref[...].astype(jnp.float32)
    norm_into(0, 0, na_ref)
    pl.semaphore_wait(bar, NZ)

    def layer(l, _):
        @pl.when(l > 0)
        def _():
            norm_into(l, 0, na_ref)

        def qkv_chunk(k):
            @pl.when(k == 0)
            def _():
                for h in range(H):
                    wq_copy(l, h).wait()
                qkv[...] = jnp.zeros_like(qkv)

            @pl.when(jnp.logical_and(l == 0, k == 0))
            def _():
                for n in range(c.NG):
                    for cp in gu_copies(n):
                        cp.start()
                for n in range(c.ND):
                    wd_copy(n).start()
            rows = pl.ds(pl.multiple_of(k * c.CKS[0], c.CKS[0]), c.CKS[0])
            qkv[...] += jnp.dot(xg[l, 0, :, kcols(0, k)], wqkv[rows, :], preferred_element_type=jnp.float32)

        def before():
            @pl.when(l == 0)
            def _():
                tables()
                lax.fori_loop(0, c.NC, lambda k, _: (kv_take(0, k), 0)[1], 0)
                wo_copy(0).start()

        gather_phase(l, 0, qkv_chunk, before)

        @pl.when(l + 1 < L)
        def _():
            for h in range(H):
                wq_copy(l + 1, h).start()
        attention()
        wo_copy(l).wait()

        def take_next(i):
            per = -(-c.NC // c.NN)
            for n in range(per):
                @pl.when(jnp.logical_and(l + 1 < L, i * per + n < c.NC))
                def _(n=n):
                    kv_take(l + 1, i * per + n)

        reduce_phase(l, 0, lambda j: jnp.dot(ctx[...], wo_b[:, ncols(j)], preferred_element_type=jnp.float32),
                     take_next)

        @pl.when(l + 1 < L)
        def _():
            wo_copy(l + 1).start()
        norm_into(l, 1, nm_ref)

        def gu_chunk(k):
            @pl.when(k == 0)
            def _():
                gacc[...] = jnp.zeros_like(gacc)
            g = l * c.NKS[1] + k
            slot = lax.rem(g, c.NG)
            for cp in gu_copies(g):
                cp.wait()
            gacc[...] += lax.dot_general(xg[l, 1, :, kcols(1, k)], gu_b[slot], (((1,), (1,)), ((), ())),
                                         preferred_element_type=jnp.float32)

            @pl.when(g + c.NG < L * c.NKS[1])
            def _():
                for cp in gu_copies(g + c.NG):
                    cp.start()

        gather_phase(l, 1, gu_chunk)
        gate = gacc[:, :c.F]
        act[...] = (gate * jax.nn.sigmoid(gate) * gacc[:, c.FP:c.FP + c.F]).astype(jnp.bfloat16)

        def down_chunk(j):
            g = l * c.NN + j
            slot = lax.rem(g, c.ND)
            wd_copy(g).wait()
            part = jnp.dot(act[...], wd_b[slot], preferred_element_type=jnp.float32)

            @pl.when(g + c.ND < L * c.NN)
            def _():
                wd_copy(g + c.ND).start()
            return part

        reduce_phase(l, 1, down_chunk)
        return 0

    lax.fori_loop(0, L, layer, 0)
    out_ref[...] = resid[...].astype(jnp.bfloat16)


def solution(mesh):
    tok_spec = P('dp', 'tp', None)
    in_specs = (tok_spec, P(), P(None, None, 'tp', None), P(), P(None, 'tp', None, None), P(), P(None, None, 'tp'), P(None, None, 'tp'), P(None, 'tp', None))

    def body(hidden, norm_attn, w_q, w_kv, w_o, norm_mlp, w_gate, w_up, w_down):
        L, D, H, E = w_q.shape
        F = w_gate.shape[2]
        T = hidden.shape[1]
        S = 8 * T
        cfg = Cfg(L, S, D, H, E, F)
        c = cfg
        bf, f32 = jnp.bfloat16, jnp.float32
        vm = pl.BlockSpec(memory_space=pltpu.VMEM)
        hb = pl.BlockSpec(memory_space=pl.ANY)
        dma = pltpu.SemaphoreType.DMA
        mk = max(c.NKS)
        scratch = [
            pltpu.VMEM((L, 2, S, D), bf),
            pltpu.VMEM((L, 2, S // 2, D), bf),
            pltpu.VMEM((L, 2, NZ, T, D), bf),
            pltpu.VMEM((S // 2, D), bf),
            pltpu.VMEM((S // 2, D), bf),
            pltpu.VMEM((S // 2, D), f32),
            pltpu.VMEM((T, D), f32),
            pltpu.VMEM((D, (H + 2) * E), bf),
            pltpu.VMEM((c.NR, c.KC, 2, 2, E), bf),
            pltpu.VMEM((c.SUB * 4, E), f32),
            pltpu.VMEM((H * E, D), bf),
            pltpu.VMEM((c.NG, c.FP + F, c.CKS[1]), bf),
            pltpu.VMEM((c.ND, F, c.CN), bf),
            pltpu.VMEM((S, (H + 2) * E), f32),
            pltpu.VMEM((S, c.FP + F), f32),
            pltpu.VMEM((S, F), bf),
            pltpu.VMEM((S, H * E), bf),
            pltpu.VMEM((T, D), bf), pltpu.VMEM((L, D), f32), pltpu.VMEM((L, D), f32),
            pltpu.VMEM((S, E), f32), pltpu.VMEM((S, E), f32), pltpu.VMEM((S, S), f32),
            dma((3,)),
            dma((H,)), dma((c.NR,)), dma, dma((c.NG, 2)), dma((c.ND,)),
            dma((L, 2, NZ, mk)), dma((L, 2, NZ, mk)), dma((5, mk)), dma((mk,)), dma((mk,)), dma((NZ, mk)),
            dma((L, 2, c.NN)), dma((L, 2, NZ, c.NN)), dma((c.NN,)), dma((NZ, c.NN)),
        ]
        out = pl.pallas_call(
            functools.partial(kernel, cfg),
            out_shape=jax.ShapeDtypeStruct((T, D), bf),
            in_specs=[hb] * 9,
            out_specs=vm,
            scratch_shapes=scratch,
            compiler_params=pltpu.CompilerParams(collective_id=0, has_side_effects=True, vmem_limit_bytes=67043328),
            name="layers",
        )(hidden[0], norm_attn, norm_mlp, jnp.transpose(w_q, (0, 2, 1, 3)), w_kv, w_o.reshape(L, H * E, D),
          jnp.transpose(w_gate, (0, 2, 1)), jnp.transpose(w_up, (0, 2, 1)), w_down)
        return out[None]

    return jax.shard_map(body, mesh=mesh, in_specs=in_specs, out_specs=tok_spec, check_vma=False)
```

time: 197 us -> 162 us (0.82)
  Pallas kernels: 190 us -> 160 us
  local copies, waits for them, and re-layouts: 4.43 us -> 1.59 us
    pallas_call x1, Pallas kernels: 190 us -> 160 us  [body(): pl.pallas_call(functools.partial(kernel, cfg), out_shape=jax.ShapeDtypeSt...]
    reshape x2 -> x0, local copies, waits for them, and re-layouts: 2.84 us -> none  [the longest x1 1.42 us: body(): norm_mlp.reshape(L, 1, D)]
where the time goes in v2:
time: 162 us; the launch traced here: 161 us
  Pallas kernels  160 us (99%)
    pallas_call x1, Pallas kernels, body(): pl.pallas_call(functools.partial(kernel, cfg), out_shape=jax.ShapeDtypeSt...  160 us

profile of v2, /device:TPU:0, one launch (start us, length us, event | category | flops | bytes accessed | tf_op | source)
XLA Modules:
  0.0 161.5 jit_solution(972312692176661741)
XLA Ops:
  0.0 159.9 %layers.1 = bf16[16,5120]{1,0:T(8,128)(2,1)} custom-call(bf16[16,5120]{1,0:T(8,128)(2,1)} %bitcast.11, f32[2,5120]{1,0:T(2,128)} %na_hbm.1, f32[2,5120]{1,0:T(2,128)} %nm_hbm.1, bf16[2,5,5120,128]{3,2,1,0:T(8,128)(2,1)} %bitcast.8, bf16[2,5120,2,8,128]{4,3,2,1,0:T(8,128)(2,1)} %wkv_hbm.1, bf16[2,640,5120]{2,1,0:T(8,128)(2,1)} %bitcast.9, ...), custom_call_target="tpu_custom_call" | custom-call | tf_op jit(solution)/shard_map/layers/pallas_call | solution.py:530
  159.9 1.6 copy.11

commit v3 on v2

--- a/solution.py
+++ b/solution.py
@@ -22,11 +22,10 @@
         self.NKS = tuple(width // n for n in self.CKS)
         self.KC = 512
         self.NC = width // self.KC
-        self.FP = -(-ff // LANES) * LANES
         self.CN = 1024
         self.NN = width // self.CN
         self.NG = 2
-        self.ND = 2
+        self.ND = 4
         self.NR = 3
         self.SUB = 128
         self.AHEAD = (4, 3)
@@ -84,7 +83,7 @@
 
     def gu_copies(g):
         l, k, slot = g // c.NKS[1], lax.rem(g, c.NKS[1]), lax.rem(g, c.NG)
-        return [pltpu.make_async_copy(w.at[l, :, kcols(1, k)], gu_b.at[slot, pl.ds(i * c.FP, c.F)], s_gu.at[slot, i])
+        return [pltpu.make_async_copy(w.at[l, :, kcols(1, k)], gu_b.at[slot, pl.ds(i * c.F, c.F)], s_gu.at[slot, i])
                 for i, w in enumerate((wg_hbm, wu_hbm))]
 
     def wd_copy(g):
@@ -388,7 +387,6 @@
         qpos = position(lax.broadcasted_iota(jnp.int32, (S, S), 0))
         mask_ref[...] = jnp.where(qpos >= kpos, 1.0, 0.0)
 
-    gu_b[:, c.F:c.FP, :] = jnp.zeros((c.NG, c.FP - c.F, c.CKS[1]), jnp.bfloat16)
     for cp in inputs:
         cp.wait()
     resid[...] = hid_ref[...].astype(jnp.float32)
@@ -456,7 +454,7 @@
             slot = lax.rem(g, c.NG)
             for cp in gu_copies(g):
                 cp.wait()
-            gacc[...] += lax.dot_general(xg[l, 1, :, kcols(1, k)], gu_b[slot], (((1,), (1,)), ((), ())),
+            gacc[...] += lax.dot_general(gu_b[slot], xg[l, 1, :, kcols(1, k)], (((1,), (1,)), ((), ())),
                                          preferred_element_type=jnp.float32)
 
             @pl.when(g + c.NG < L * c.NKS[1])
@@ -465,8 +463,8 @@
                     cp.start()
 
         gather_phase(l, 1, gu_chunk)
-        gate = gacc[:, :c.F]
-        act[...] = (gate * jax.nn.sigmoid(gate) * gacc[:, c.FP:c.FP + c.F]).astype(jnp.bfloat16)
+        gate = gacc[:c.F]
+        act[...] = (gate * jax.nn.sigmoid(gate) * gacc[c.F:]).T.astype(jnp.bfloat16)
 
         def down_chunk(j):
             g = l * c.NN + j
@@ -514,10 +512,10 @@
             pltpu.VMEM((c.NR, c.KC, 2, 2, E), bf),
             pltpu.VMEM((c.SUB * 4, E), f32),
             pltpu.VMEM((H * E, D), bf),
-            pltpu.VMEM((c.NG, c.FP + F, c.CKS[1]), bf),
+            pltpu.VMEM((c.NG, 2 * F, c.CKS[1]), bf),
             pltpu.VMEM((c.ND, F, c.CN), bf),
             pltpu.VMEM((S, (H + 2) * E), f32),
-            pltpu.VMEM((S, c.FP + F), f32),
+            pltpu.VMEM((2 * F, S), f32),
             pltpu.VMEM((S, F), bf),
             pltpu.VMEM((S, H * E), bf),
             pltpu.VMEM((T, D), bf), pltpu.VMEM((L, D), f32), pltpu.VMEM((L, D), f32),

time: 162 us -> 156 us (0.963)
  Pallas kernels: 160 us -> 155 us
    pallas_call x1, Pallas kernels: 160 us -> 155 us  [body(): pl.pallas_call(functools.partial(kernel, cfg), out_shape=jax.ShapeDtypeSt...]
where the time goes in v3:
time: 156 us
  Pallas kernels  155 us (99%)
  local copies, waits for them, and re-layouts  1.59 us (1%)
    pallas_call x1, Pallas kernels, body(): pl.pallas_call(functools.partial(kernel, cfg), out_shape=jax.ShapeDtypeSt...  155 us

profile of v3, /device:TPU:0, one launch (start us, length us, event | category | flops | bytes accessed | tf_op | source)
XLA Modules:
  0.0 156.2 jit_solution(8335097905494860782)
XLA Ops:
  0.0 154.6 %layers.1 = bf16[16,5120]{1,0:T(8,128)(2,1)} custom-call(bf16[16,5120]{1,0:T(8,128)(2,1)} %bitcast.11, f32[2,5120]{1,0:T(2,128)} %na_hbm.1, f32[2,5120]{1,0:T(2,128)} %nm_hbm.1, bf16[2,5,5120,128]{3,2,1,0:T(8,128)(2,1)} %bitcast.8, bf16[2,5120,2,8,128]{4,3,2,1,0:T(8,128)(2,1)} %wkv_hbm.1, bf16[2,640,5120]{2,1,0:T(8,128)(2,1)} %bitcast.9, ...), custom_call_target="tpu_custom_call" | custom-call | tf_op jit(solution)/shard_map/layers/pallas_call | solution.py:528
  154.7 1.6 %copy.11 = bf16[1,16,5120]{2,1,0:T(8,128)(2,1)} copy(bf16[1,16,5120]{2,1,0:T(8,128)(2,1)} %bitcast.10) | data formatting | bytes 327680

commit v4 on v3

--- a/solution.py
+++ b/solution.py
@@ -30,7 +30,7 @@
         self.SUB = 128
         self.AHEAD = (4, 3)
         self.LF, self.LP, self.LC = 0, 1, 2
-        self.RP, self.RA, self.RB, self.RM, self.RS = 2, 3, 4, 4, 6
+        self.RP, self.RA, self.RB, self.RM, self.RS = 2, 3, 4, 4, 9
 
 
 def kernel(cfg, hid_hbm, na_hbm, nm_hbm, wq_hbm, wkv_hbm, wo_hbm, wg_hbm, wu_hbm, wd_hbm, out_ref,
@@ -92,8 +92,10 @@
 
     bar = pltpu.get_barrier_semaphore()
     pl.semaphore_signal(bar, inc=1, device_id=(dp, partner), device_id_type=MESH)
-    for d in range(1, NZ):
-        pl.semaphore_signal(bar, inc=1, device_id=(dp, chip(lax.rem(z + d, NZ))), device_id_type=MESH)
+    for dz in (1, -1, 2, -2):
+        @pl.when(jnp.logical_and(z + dz >= 0, z + dz < NZ))
+        def _(dz=dz):
+            pl.semaphore_signal(bar, inc=1, device_id=(dp, chip(z + dz)), device_id_type=MESH)
 
     inputs = [pltpu.make_async_copy(a, b, s_in.at[i])
               for i, (a, b) in enumerate(((hid_hbm, hid_ref), (na_hbm, na_ref), (nm_hbm, nm_ref)))]
@@ -289,20 +291,20 @@
             def _():
                 stage_pair(i - c.RP)
 
+            @pl.when(jnp.logical_and(i >= c.RA, i < c.NN + c.RA))
+            def _():
+                send(i - c.RA, (2, 1), lambda d: z == (0 if d == 2 else 3))
+
+            @pl.when(jnp.logical_and(i >= c.RB, i < c.NN + c.RB))
+            def _():
+                send(i - c.RB, (1, 2), lambda d: z == (0 if d == 1 else 3))
+
+            @pl.when(jnp.logical_and(i >= c.RM, i < c.NN + c.RM))
+            def _():
+                stage_mid(i - c.RM)
+
             if beside is not None:
                 beside(i)
-
-            @pl.when(jnp.logical_and(i >= c.RA, i < c.NN + c.RA))
-            def _():
-                send(i - c.RA, (2, 1), lambda d: z == (0 if d == 2 else 3))
-
-            @pl.when(jnp.logical_and(i >= c.RB, i < c.NN + c.RB))
-            def _():
-                send(i - c.RB, (1, 2), lambda d: z == (0 if d == 1 else 3))
-
-            @pl.when(jnp.logical_and(i >= c.RM, i < c.NN + c.RM))
-            def _():
-                stage_mid(i - c.RM)
 
             @pl.when(i >= c.RS)
             def _():
@@ -391,7 +393,7 @@
         cp.wait()
     resid[...] = hid_ref[...].astype(jnp.float32)
     norm_into(0, 0, na_ref)
-    pl.semaphore_wait(bar, NZ)
+    pl.semaphore_wait(bar, jnp.where(middle, NZ, NZ - 1))
 
     def layer(l, _):
         @pl.when(l > 0)
@@ -432,11 +434,9 @@
         wo_copy(l).wait()
 
         def take_next(i):
-            per = -(-c.NC // c.NN)
-            for n in range(per):
-                @pl.when(jnp.logical_and(l + 1 < L, i * per + n < c.NC))
-                def _(n=n):
-                    kv_take(l + 1, i * per + n)
+            @pl.when(jnp.logical_and(l + 1 < L, i == c.RS - 1))
+            def _():
+                lax.fori_loop(0, c.NC, lambda k, _: (kv_take(l + 1, k), 0)[1], 0)
 
         reduce_phase(l, 0, lambda j: jnp.dot(ctx[...], wo_b[:, ncols(j)], preferred_element_type=jnp.float32),
                      take_next)
@@ -464,7 +464,7 @@
 
         gather_phase(l, 1, gu_chunk)
         gate = gacc[:c.F]
-        act[...] = (gate * jax.nn.sigmoid(gate) * gacc[c.F:]).T.astype(jnp.bfloat16)
+        act[...] = (gate * jax.nn.sigmoid(gate) * gacc[c.F:]).astype(jnp.bfloat16).T
 
         def down_chunk(j):
             g = l * c.NN + j

time: 156 us -> 151 us (0.968)
  Pallas kernels: 155 us -> 149 us
    pallas_call x1, Pallas kernels: 155 us -> 149 us  [body(): pl.pallas_call(functools.partial(kernel, cfg), out_shape=jax.ShapeDtypeSt...]
where the time goes in v4:
time: 151 us
  Pallas kernels  149 us (99%)
  local copies, waits for them, and re-layouts  1.59 us (1%)
    pallas_call x1, Pallas kernels, body(): pl.pallas_call(functools.partial(kernel, cfg), out_shape=jax.ShapeDtypeSt...  149 us

profile of v4, /device:TPU:0, one launch (start us, length us, event | category | flops | bytes accessed | tf_op | source)
XLA Modules:
  0.0 150.8 jit_solution(16757149061568283533)
XLA Ops:
  0.0 149.2 %layers.1 = bf16[16,5120]{1,0:T(8,128)(2,1)} custom-call(bf16[16,5120]{1,0:T(8,128)(2,1)} %bitcast.11, f32[2,5120]{1,0:T(2,128)} %na_hbm.1, f32[2,5120]{1,0:T(2,128)} %nm_hbm.1, bf16[2,5,5120,128]{3,2,1,0:T(8,128)(2,1)} %bitcast.8, bf16[2,5120,2,8,128]{4,3,2,1,0:T(8,128)(2,1)} %wkv_hbm.1, bf16[2,640,5120]{2,1,0:T(8,128)(2,1)} %bitcast.9, ...), custom_call_target="tpu_custom_call" | custom-call | tf_op jit(solution)/shard_map/layers/pallas_call | solution.py:528
  149.2 1.6 %copy.11 = bf16[1,16,5120]{2,1,0:T(8,128)(2,1)} copy(bf16[1,16,5120]{2,1,0:T(8,128)(2,1)} %bitcast.10) | data formatting | bytes 327680
